TPU v7x, 32 devices: a whole 2x2x4 slice. The times are simulated.
32 devices in a mesh: groups: 2 (over y), seq: 4 (over z), head: 2 (over x), rep: 2 (over core).
Axes of the slice: x: 2, y: 2, z: 4, core: 2. Of those that a mesh axis runs over, the one named last changes fastest.
Arguments:
- queries: bfloat16 [128, 64, 128], P(('groups', 'seq', 'rep'), 'head'), parts along dimension 0, may hold values from -256 to 256
- page_owner: int32 [128, 128], P(('groups', 'seq', 'rep')), parts along dimension 0, may hold values from -1 to 3, as said below
- page_slot: int32 [128, 128], P(('groups', 'seq', 'rep')), parts along dimension 0, may hold values from -1 to 63, as said below
- lengths: int32 [128], P(('groups', 'seq', 'rep')), parts along dimension 0, may hold values from 1 to 16384, as said below
- keys: bfloat16 [1024, 8, 128, 128], P(('groups', 'seq', 'rep'), 'head'), parts along dimension 0, may hold values from -24 to 24
- values: bfloat16 [1024, 8, 128, 128], P(('groups', 'seq', 'rep'), 'head'), parts along dimension 0, may hold values from -6 to 6
Outputs:
- attended: bfloat16 [128, 64, 128], P(('groups', 'seq', 'rep'), 'head'), parts along dimension 0
There are 2 independent parts, one for each index of `groups`. A program takes and returns all parts, laid end to end along the dimension named above; each array names one. Nothing has to cross between parts.
Inputs may be any that keep to these rules, and one draw needn't show every extreme that they name: `page_owner`: for j below ceil(lengths[r] / 128) the seq index of the device, among those of r's half (r // 8) % 2, whose pool holds page j of r; -1 for later j. `page_slot`: the page's slot in that pool, -1 where page_owner is -1. No slot of a pool holds two pages; in each half, some device's pool has all 64 slots in use. `lengths`: in each half some request has the most.
All inputs are finite; a program needn't handle non-finite values.
Results may differ from a plain program's by a relative error of at most 0.0041.
Values may be sent and summed in bfloat16 or wider, within the bound.
A program may use at most 64 MiB of HBM per device.

v0:
```python
import math
import jax
import jax.numpy as jnp
from jax import lax
from jax.sharding import PartitionSpec as P

masked_score = -1e30


def on_device(queries, page_owner, page_slot, lengths, keys, values):
    rows_own = queries.shape[0]
    head_count = queries.shape[1]
    head_width = queries.shape[2]
    pool_size = keys.shape[0]
    kv_heads = keys.shape[1]
    page_tokens = keys.shape[2]
    group_size = head_count // kv_heads
    most_pages = page_owner.shape[1]
    page_index = jnp.arange(most_pages, dtype=jnp.int32)
    all_queries, all_owner, all_slot, all_length = (
        lax.all_gather(queries, "seq", axis=0, tiled=True),
        lax.all_gather(page_owner, "seq", axis=0, tiled=True),
        lax.all_gather(page_slot, "seq", axis=0, tiled=True),
        lax.all_gather(lengths, "seq", axis=0, tiled=True),
    )
    live_count = jnp.clip(all_length[:, None] - page_index[None, :] * page_tokens, 0, page_tokens)
    rows_half = all_queries.shape[0]
    seq_index = lax.axis_index("seq")
    held_here = (all_owner == seq_index) & (live_count > 0)
    slot_index = jnp.arange(pool_size, dtype=jnp.int32)
    matches = held_here[None, :, :] & (all_slot[None, :, :] == slot_index[:, None, None])
    slot_owner = jnp.any(matches, axis=2)
    slot_tokens = jnp.sum(jnp.where(matches, live_count[None, :, :], 0), axis=(1, 2))
    picker = slot_owner.astype(jnp.bfloat16)
    flat_queries = all_queries.reshape(rows_half, head_count * head_width)
    slot_queries = jnp.dot(picker, flat_queries, preferred_element_type=jnp.float32)
    slot_queries = slot_queries.astype(jnp.bfloat16).reshape(
        pool_size, kv_heads, group_size, head_width
    )
    score_scale = 1.0 / math.sqrt(head_width)
    scores = (
        jnp.einsum("pkgd,pktd->pkgt", slot_queries, keys, preferred_element_type=jnp.float32)
        * score_scale
    )
    token_index = jnp.arange(page_tokens, dtype=jnp.int32)
    live_tokens = (token_index[None, :] < slot_tokens[:, None])[:, None, None, :]
    scores = jnp.where(live_tokens, scores, masked_score)
    page_max = jnp.max(scores, axis=3)
    weights = jnp.where(live_tokens, jnp.exp(scores - page_max[..., None]), 0.0)
    page_sum = jnp.sum(weights, axis=3)
    page_out = jnp.einsum(
        "pkgt,pktd->pkgd", weights.astype(jnp.bfloat16), values, preferred_element_type=jnp.float32
    )
    linked = slot_owner.T[:, :, None, None]
    request_max = jnp.max(jnp.where(linked, page_max[None], masked_score), axis=1)
    rescale = jnp.where(
        linked, jnp.exp(jnp.minimum(page_max[None] - request_max[:, None], 0.0)), 0.0
    )
    request_sum = jnp.sum(rescale * page_sum[None], axis=1)
    request_out = jnp.einsum("rpkg,pkgd->rkgd", rescale, page_out, precision=lax.Precision.HIGHEST)
    got_max, got_sum, got_out = (
        lax.all_to_all(request_max, "seq", split_axis=0, concat_axis=0, tiled=True),
        lax.all_to_all(request_sum, "seq", split_axis=0, concat_axis=0, tiled=True),
        lax.all_to_all(request_out, "seq", split_axis=0, concat_axis=0, tiled=True),
    )
    sources = rows_half // rows_own
    got_max = got_max.reshape((sources, rows_own) + got_max.shape[1:])
    got_sum = got_sum.reshape((sources, rows_own) + got_sum.shape[1:])
    got_out = got_out.reshape((sources, rows_own) + got_out.shape[1:])
    overall = jnp.max(got_max, axis=0)
    source_scale = jnp.exp(got_max - overall[None])
    own_sum = jnp.sum(source_scale * got_sum, axis=0)
    own_out = jnp.sum(source_scale[..., None] * got_out, axis=0)
    attended = own_out / own_sum[..., None]
    return attended.astype(jnp.bfloat16).reshape(rows_own, head_count, head_width)


def solution(mesh):
    placed = (
        P(("groups", "seq", "rep"), "head", None),
        P(("groups", "seq", "rep"), None),
        P(("groups", "seq", "rep"), None),
        P(("groups", "seq", "rep")),
        P(("groups", "seq", "rep"), "head", None, None),
        P(("groups", "seq", "rep"), "head", None, None),
    )
    return jax.shard_map(
        on_device,
        mesh=mesh,
        in_specs=placed,
        out_specs=P(("groups", "seq", "rep"), "head", None),
        check_vma=False,
    )
```

profile of v0, /device:TPU:0, one launch (start us, length us, event | category | flops | bytes accessed | tf_op | source)
XLA Modules:
  0.0 100.2 jit_solution(10780645562737073349)
XLA Ops:
  0.0 1.2 %dynamic-slice = u32[1]{0:T(128)} dynamic-slice(u32[32]{0:T(128)} %constant.28, u32[]{:T(128)S(6)} %add), dynamic_slice_sizes={1} | dynamic-slice | bytes 12
  1.9 0.9 dynamic-update-slice
  2.8 9.9 %all-reduce = s32[32]{0:T(128)S(1)} all-reduce(s32[32]{0:T(128)S(1)} %dynamic-update-slice), channel_id=1, replica_groups=mesh['groups'=2,'seq'=4,'head'=2,'rep'=2] {'seq'}, use_global_device_ids=true, to_apply=%add | all-reduce | flops 32 | bytes 256
  12.7 13.3 %all_gather.12 = s32[32,128]{1,0:T(8,128)S(1)} all-gather(s32[8,128]{1,0:T(8,128)} %param.7), channel_id=1, replica_groups=mesh['groups'=2,'seq'=4,'head'=2,'rep'=2] {'seq'}, dimensions={0}, use_global_device_ids=true | all-gather | bytes 20480 | tf_op jit(solution)/shard_map/all_gather | solution.py:22
  26.0 13.3 %all_gather.14 = s32[32,128]{1,0:T(8,128)S(1)} all-gather(s32[8,128]{1,0:T(8,128)} %param.8), channel_id=1, replica_groups=mesh['groups'=2,'seq'=4,'head'=2,'rep'=2] {'seq'}, dimensions={0}, use_global_device_ids=true | all-gather | bytes 20480 | tf_op jit(solution)/shard_map/all_gather | solution.py:23
  39.4 0.1 subtract_clamp_fusion
  39.4 0.1 compare_and_fusion
  39.5 1.2 %fusion.4 = pred[64,32]{1,0:T(8,128)(4,1)S(1)} fusion(s32[32,128]{1,0:T(8,128)S(1)} %all_gather.14, pred[32,128]{1,0:T(8,128)(4,1)S(1)} %compare_and_fusion), kind=kLoop, calls=%fused_computation.10 | loop fusion | flops 784384 | bytes 22528 | tf_op jit(solution)/shard_map/reduce_or | solution.py:32
  40.7 1.2 %select_reduce_fusion = s32[64]{0:T(128)S(1)} fusion(s32[32,128]{1,0:T(8,128)S(1)} %subtract_clamp_fusion, s32[32,128]{1,0:T(8,128)S(1)} %all_gather.14, pred[32,128]{1,0:T(8,128)(4,1)S(1)} %compare_and_fusion), kind=kLoop, calls=%fused_computation.7 | loop fusion | flops 1048512 | bytes 37120 | tf_op jit(solution)/shard_map/reduce_sum | solution.py:33
  41.9 0.1 iota_compare_fusion.1
  42.0 14.0 %all_gather.15 = bf16[32,32,128]{2,1,0:T(8,128)(2,1)S(1)} all-gather(bf16[8,32,128]{2,1,0:T(8,128)(2,1)} %param.6), channel_id=1, replica_groups=mesh['groups'=2,'seq'=4,'head'=2,'rep'=2] {'seq'}, dimensions={0}, use_global_device_ids=true | all-gather | bytes 327680 | tf_op jit(solution)/shard_map/all_gather | solution.py:21
  56.0 0.3 fusion.1
  56.3 0.1 copy.43
  56.4 6.9 %fusion.22 = (f32[64,4,8]{2,1,0:T(4,128)S(1)}, f32[64,4,8,128]{3,2,1,0:T(8,128)S(1)}) fusion(bf16[64,4,8,128]{3,2,1,0:T(8,128)(2,1)S(1)} %bitcast.21, bf16[64,4,128,128]{3,2,1,0:T(8,128)(2,1)} %param.10, pred[64,128]{1,0:T(8,128)(4,1)S(1)} %iota_compare_fusion.1), kind=kOutput, calls=%fused_computation.38 | convolution fusion | flops 67893248 | bytes 9977856 | tf_op jit(solution)/shard_map/pkgd,pktd->pkgt/dot_general | solution.py:42
  63.3 0.1 copy.30
  63.4 0.8 fusion.5
  64.2 0.1 copy.37
  64.3 0.1 copy.29
  64.4 0.2 select_reduce_fusion.1
  64.6 0.4 multiply_reduce_fusion
  65.0 0.1 copy.38
  65.1 0.7 reshape.94
  65.8 3.2 %all-to-all-start.2 = ((f32[4,1,256]{2,1,0:T(1,128)}), f32[4,1,256]{2,1,0:T(1,128)S(1)}, u32[]{:S(2)}, u32[]{:S(2)}) async-start(f32[4,1,256]{2,1,0:T(1,128)} %reshape.94), calls=%async_computation.2 | async-start | bytes 8192 | tf_op jit(solution)/shard_map/all_to_all | solution.py:63
  69.1 4.7 %fusion.7 = f32[64,4,8,128]{3,2,1,0:T(8,128)S(1)} fusion(bf16[64,4,128,128]{3,2,1,0:T(8,128)(2,1)} %param.11, f32[64,4,8,128]{3,2,1,0:T(8,128)S(1)} %get-tuple-element.8, f32[64,4,8]{2,1,0:T(4,128)S(1)} %get-tuple-element.7, pred[64,128]{1,0:T(8,128)(4,1)S(1)} %iota_compare_fusion.1), kind=kOutput, calls=%fused_computation.13 | convolution fusion | flops 67895296 | bytes 10502144 | tf_op jit(solution)/shard_map/pkgt,pktd->pkgd/dot_general | solution.py:51
  73.8 0.1 copy.31
  73.9 0.7 reshape.92
  74.6 0.0 all-to-all-done.2
  74.6 5.0 %all-to-all-start = ((f32[4,1,256]{2,1,0:T(1,128)}), f32[4,1,256]{2,1,0:T(1,128)S(1)}, u32[]{:S(2)}, u32[]{:S(2)}) async-start(f32[4,1,256]{2,1,0:T(1,128)} %reshape.92), calls=%async_computation | async-start | bytes 8192 | tf_op jit(solution)/shard_map/all_to_all | solution.py:62
  79.7 1.6 %convolution_bitcast_fusion = f32[32,4,8,128]{3,0,2,1:T(8,128)S(1)} fusion(f32[64,4,8,128]{3,2,1,0:T(8,128)S(1)} %fusion.7, f32[32,4,8]{0,2,1:T(8,128)S(1)} %select_reduce_fusion.1, f32[64,4,8]{0,2,1:T(8,128)S(1)} %copy.30, pred[32,64]{1,0:T(8,128)(4,1)S(1)} %copy.29), kind=kOutput, calls=%fused_computation.4 | convolution fusion | flops 100859904 | bytes 1587200 | tf_op jit(solution)/shard_map/rpkg,pkgd->rkgd/dot_general | solution.py:60
  81.3 1.1 %copy.35 = f32[32,4,8,128]{3,2,1,0:T(8,128)} copy(f32[32,4,8,128]{3,0,2,1:T(8,128)S(1)} %convolution_bitcast_fusion) | data formatting | bytes 1048576 | tf_op jit(solution)/shard_map/rpkg,pkgd->rkgd/transpose | solution.py:60
  82.4 2.9 %all-to-all-done = f32[4,1,256]{2,1,0:T(1,128)S(1)} async-done(((f32[4,1,256]{2,1,0:T(1,128)}), f32[4,1,256]{2,1,0:T(1,128)S(1)}, u32[]{:S(2)}, u32[]{:S(2)}) %all-to-all-start) | async-done | bytes 4128 | tf_op jit(solution)/shard_map/all_to_all | solution.py:62
  85.3 3.5 %all-to-all-start.1 = ((f32[32,4,8,128]{3,2,1,0:T(8,128)}), f32[32,4,8,128]{3,2,1,0:T(8,128)S(1)}, u32[]{:S(2)}, u32[]{:S(2)}) async-start(f32[32,4,8,128]{3,2,1,0:T(8,128)} %copy.35), calls=%async_computation.1 | async-start | bytes 1048576 | tf_op jit(solution)/shard_map/all_to_all | solution.py:64
  88.8 0.5 broadcast.55
  89.3 0.7 reduce
  90.0 0.1 reshape.95
  90.1 0.1 copy.39
  90.2 0.7 reduce.1
  90.9 0.1 reshape.93
  91.0 0.1 copy.33
  91.2 0.1 copy.32
  91.3 0.1 multiply_reduce_fusion.1
  91.3 0.1 copy.40
  91.4 7.7 %all-to-all-done.1 = f32[32,4,8,128]{3,2,1,0:T(8,128)S(1)} async-done(((f32[32,4,8,128]{3,2,1,0:T(8,128)}), f32[32,4,8,128]{3,2,1,0:T(8,128)S(1)}, u32[]{:S(2)}, u32[]{:S(2)}) %all-to-all-start.1) | async-done | bytes 524320 | tf_op jit(solution)/shard_map/all_to_all | solution.py:64
  99.1 0.3 fusion.9
  99.4 0.7 fusion.19
  (3 shorter events, 0.0 us)
Async XLA Ops:
  65.8 8.8 %all-to-all-start.2 = ((f32[4,1,256]{2,1,0:T(1,128)}), f32[4,1,256]{2,1,0:T(1,128)S(1)}, u32[]{:S(2)}, u32[]{:S(2)}) async-start(f32[4,1,256]{2,1,0:T(1,128)} %reshape.94), calls=%async_computation.2 | async-start | bytes 8192 | tf_op jit(solution)/shard_map/all_to_all | solution.py:63
  74.6 10.7 %all-to-all-start = ((f32[4,1,256]{2,1,0:T(1,128)}), f32[4,1,256]{2,1,0:T(1,128)S(1)}, u32[]{:S(2)}, u32[]{:S(2)}) async-start(f32[4,1,256]{2,1,0:T(1,128)} %reshape.92), calls=%async_computation | async-start | bytes 8192 | tf_op jit(solution)/shard_map/all_to_all | solution.py:62
  85.3 13.7 %all-to-all-start.1 = ((f32[32,4,8,128]{3,2,1,0:T(8,128)}), f32[32,4,8,128]{3,2,1,0:T(8,128)S(1)}, u32[]{:S(2)}, u32[]{:S(2)}) async-start(f32[32,4,8,128]{3,2,1,0:T(8,128)} %copy.35), calls=%async_computation.1 | async-start | bytes 1048576 | tf_op jit(solution)/shard_map/all_to_all | solution.py:64
where the time goes:
time: 101 us; the launch traced here: 100 us
  blocking collectives  50.6 us (50%)
  matrix products  13.6 us (13%)
  starting transfers between devices  11.8 us (12%)
  waiting for transfers between devices  10.6 us (10%)
  other arithmetic  6.56 us (6%)
  local copies, waits for them, and re-layouts  6.25 us (6%)
    all_gather x1, blocking collectives, on_device(): lax.all_gather(queries, 'seq', axis=0, tiled=True)  14 us
    all_gather x1, blocking collectives, on_device(): lax.all_gather(page_slot, 'seq', axis=0, tiled=True)  13.3 us
    all_gather x1, blocking collectives, on_device(): lax.all_gather(page_owner, 'seq', axis=0, tiled=True)  13.3 us
    unnamed x1, blocking collectives  9.92 us
    all_to_all x1, waiting for transfers between devices, on_device(): lax.all_to_all(request_out, 'seq', split_axis=0, concat_axis=0, tiled=True)  7.67 us
    dot_general x1, matrix products, on_device(): jnp.einsum('pkgd,pktd->pkgt', slot_queries, keys, preferred_element_type=...  6.94 us
    all_to_all x1, starting transfers between devices, on_device(): lax.all_to_all(request_max, 'seq', split_axis=0, concat_axis=0, tiled=True)  5.04 us
    dot_general x1, matrix products, on_device(): jnp.einsum('pkgt,pktd->pkgd', weights.astype(jnp.bfloat16), values, prefe...  4.72 us
  transfers between devices with their start and end apart: 3, of which 2 were waited for; matrix products, arithmetic and copies ran while one was open for 11% of the time, Pallas kernels for 0%

commit v1 on v0

--- a/solution.py
+++ b/solution.py
@@ -18,7 +18,9 @@
     most_pages = page_owner.shape[1]
     page_index = jnp.arange(most_pages, dtype=jnp.int32)
     all_queries, all_owner, all_slot, all_length = (
-        lax.all_gather(queries, "seq", axis=0, tiled=True),
+        jnp.concatenate(
+            lax.all_to_all(jnp.stack([queries] * lax.axis_size("seq")), "seq", 0, 0), axis=0
+        ),
         lax.all_gather(page_owner, "seq", axis=0, tiled=True),
         lax.all_gather(page_slot, "seq", axis=0, tiled=True),
         lax.all_gather(lengths, "seq", axis=0, tiled=True),

time: 101 us -> 94 us (0.931)
  blocking collectives: 50.6 us -> 35.5 us
  starting transfers between devices: 11.8 us -> 18.7 us
  local copies, waits for them, and re-layouts: 6.25 us -> 7.82 us
    all_gather x1 -> x0, blocking collectives: 14 us -> none  [on_device(): lax.all_gather(queries, 'seq', axis=0, tiled=True)]
    all_to_all x0 -> x1, starting transfers between devices: none -> 6.35 us  [on_device(): lax.all_to_all(jnp.stack([queries] * lax.axis_size('seq')), 'seq', 0, 0)]
    another operation x0 -> x1, local copies, waits for them, and re-layouts: none -> 1.57 us  [on_device(): jnp.stack([queries] * lax.axis_size('seq'))]
    unnamed x1, blocking collectives: 9.92 us -> 8.78 us
  transfers between devices with their start and end apart: 3 -> 4, of which waited for: 2 -> 2; matrix products, arithmetic and copies ran while one was open for 11% -> 17% of each run, Pallas kernels for 0% -> 0%
where the time goes in v1:
time: 94 us; the launch traced here: 93.5 us
  blocking collectives  35.5 us (38%)
  starting transfers between devices  18.7 us (20%)
  matrix products  13.6 us (14%)
  waiting for transfers between devices  10.6 us (11%)
  local copies, waits for them, and re-layouts  7.82 us (8%)
  other arithmetic  6.57 us (7%)
    all_gather x1, blocking collectives, on_device(): lax.all_gather(page_owner, 'seq', axis=0, tiled=True)  13.3 us
    all_gather x1, blocking collectives, on_device(): lax.all_gather(page_slot, 'seq', axis=0, tiled=True)  13.3 us
    unnamed x1, blocking collectives  8.78 us
    all_to_all x1, waiting for transfers between devices, on_device(): lax.all_to_all(request_out, 'seq', split_axis=0, concat_axis=0, tiled=True)  7.71 us
    dot_general x1, matrix products, on_device(): jnp.einsum('pkgd,pktd->pkgt', slot_queries, keys, preferred_element_type=...  6.94 us
    all_to_all x1, starting transfers between devices, on_device(): lax.all_to_all(jnp.stack([queries] * lax.axis_size('seq')), 'seq', 0, 0)  6.35 us
    all_to_all x1, starting transfers between devices, on_device(): lax.all_to_all(request_max, 'seq', split_axis=0, concat_axis=0, tiled=True)  5.04 us
    dot_general x1, matrix products, on_device(): jnp.einsum('pkgt,pktd->pkgd', weights.astype(jnp.bfloat16), values, prefe...  4.72 us
  transfers between devices with their start and end apart: 4, of which 2 were waited for; matrix products, arithmetic and copies ran while one was open for 17% of the time, Pallas kernels for 0%

profile of v1, /device:TPU:0, one launch (start us, length us, event | category | flops | bytes accessed | tf_op | source)
XLA Modules:
  0.0 93.5 jit_solution(5887006460311330490)
XLA Ops:
  0.0 1.6 %stack.2 = bf16[4,8,32,128]{3,2,1,0:T(8,128)(2,1)} broadcast(bf16[8,32,128]{2,1,0:T(8,128)(2,1)} %param.6), dimensions={1,2,3} | broadcast | bytes 327680 | tf_op jit(solution)/shard_map/stack | solution.py:22
  1.6 6.3 %all-to-all-start = ((bf16[4,8,32,128]{3,2,1,0:T(8,128)(2,1)}), bf16[4,8,32,128]{3,2,1,0:T(8,128)(2,1)S(1)}, u32[]{:S(2)}, u32[]{:S(2)}) async-start(bf16[4,8,32,128]{3,2,1,0:T(8,128)(2,1)} %stack.2), calls=%async_computation | async-start | bytes 524288 | tf_op jit(solution)/shard_map/all_to_all | solution.py:22
  7.9 1.2 %dynamic-slice = u32[1]{0:T(128)} dynamic-slice(u32[32]{0:T(128)} %constant.28, u32[]{:T(128)S(6)} %add), dynamic_slice_sizes={1} | dynamic-slice | bytes 12
  9.8 0.9 dynamic-update-slice
  10.7 8.8 %all-reduce = s32[32]{0:T(128)S(1)} all-reduce(s32[32]{0:T(128)S(1)} %dynamic-update-slice), channel_id=1, replica_groups=mesh['groups'=2,'seq'=4,'head'=2,'rep'=2] {'seq'}, use_global_device_ids=true, to_apply=%add | all-reduce | flops 32 | bytes 256
  19.5 13.3 %all_gather.9 = s32[32,128]{1,0:T(8,128)S(1)} all-gather(s32[8,128]{1,0:T(8,128)} %param.7), channel_id=1, replica_groups=mesh['groups'=2,'seq'=4,'head'=2,'rep'=2] {'seq'}, dimensions={0}, use_global_device_ids=true | all-gather | bytes 20480 | tf_op jit(solution)/shard_map/all_gather | solution.py:24
  32.8 13.3 %all_gather.11 = s32[32,128]{1,0:T(8,128)S(1)} all-gather(s32[8,128]{1,0:T(8,128)} %param.8), channel_id=1, replica_groups=mesh['groups'=2,'seq'=4,'head'=2,'rep'=2] {'seq'}, dimensions={0}, use_global_device_ids=true | all-gather | bytes 20480 | tf_op jit(solution)/shard_map/all_gather | solution.py:25
  46.1 0.1 subtract_clamp_fusion
  46.2 0.1 compare_and_fusion
  46.3 1.2 %fusion.4 = pred[64,32]{1,0:T(8,128)(4,1)S(1)} fusion(s32[32,128]{1,0:T(8,128)S(1)} %all_gather.11, pred[32,128]{1,0:T(8,128)(4,1)S(1)} %compare_and_fusion), kind=kLoop, calls=%fused_computation.10 | loop fusion | flops 784384 | bytes 22528 | tf_op jit(solution)/shard_map/reduce_or | solution.py:34
  47.5 0.1 copy.29
  47.6 1.2 %select_reduce_fusion = s32[64]{0:T(128)S(1)} fusion(s32[32,128]{1,0:T(8,128)S(1)} %subtract_clamp_fusion, s32[32,128]{1,0:T(8,128)S(1)} %all_gather.11, pred[32,128]{1,0:T(8,128)(4,1)S(1)} %compare_and_fusion), kind=kLoop, calls=%fused_computation.7 | loop fusion | flops 1048512 | bytes 37120 | tf_op jit(solution)/shard_map/reduce_sum | solution.py:35
  48.8 0.1 iota_compare_fusion.1
  48.9 0.0 all-to-all-done
  48.9 0.3 fusion.1
  49.2 0.1 copy.43
  49.3 6.9 %fusion.22 = (f32[64,4,8]{2,1,0:T(4,128)S(1)}, f32[64,4,8,128]{3,2,1,0:T(8,128)S(1)}) fusion(bf16[64,4,8,128]{3,2,1,0:T(8,128)(2,1)S(1)} %bitcast.22, bf16[64,4,128,128]{3,2,1,0:T(8,128)(2,1)} %param.10, pred[64,128]{1,0:T(8,128)(4,1)S(1)} %iota_compare_fusion.1), kind=kOutput, calls=%fused_computation.38 | convolution fusion | flops 67893248 | bytes 9977856 | tf_op jit(solution)/shard_map/pkgd,pktd->pkgt/dot_general | solution.py:44
  56.2 0.1 copy.30
  56.3 0.8 fusion.5
  57.1 0.1 copy.37
  57.2 0.2 select_reduce_fusion.1
  57.4 0.4 multiply_reduce_fusion
  57.8 0.1 copy.38
  57.9 0.7 reshape.92
  58.6 3.2 %all-to-all-start.3 = ((f32[4,1,256]{2,1,0:T(1,128)}), f32[4,1,256]{2,1,0:T(1,128)S(1)}, u32[]{:S(2)}, u32[]{:S(2)}) async-start(f32[4,1,256]{2,1,0:T(1,128)} %reshape.92), calls=%async_computation.3 | async-start | bytes 8192 | tf_op jit(solution)/shard_map/all_to_all | solution.py:65
  61.9 4.7 %fusion.7 = f32[64,4,8,128]{3,2,1,0:T(8,128)S(1)} fusion(bf16[64,4,128,128]{3,2,1,0:T(8,128)(2,1)} %param.11, f32[64,4,8,128]{3,2,1,0:T(8,128)S(1)} %get-tuple-element.8, f32[64,4,8]{2,1,0:T(4,128)S(1)} %get-tuple-element.7, pred[64,128]{1,0:T(8,128)(4,1)S(1)} %iota_compare_fusion.1), kind=kOutput, calls=%fused_computation.13 | convolution fusion | flops 67895296 | bytes 10502144 | tf_op jit(solution)/shard_map/pkgt,pktd->pkgd/dot_general | solution.py:53
  66.6 0.1 copy.31
  66.7 0.7 reshape.90
  67.4 0.0 all-to-all-done.3
  67.4 5.0 %all-to-all-start.1 = ((f32[4,1,256]{2,1,0:T(1,128)}), f32[4,1,256]{2,1,0:T(1,128)S(1)}, u32[]{:S(2)}, u32[]{:S(2)}) async-start(f32[4,1,256]{2,1,0:T(1,128)} %reshape.90), calls=%async_computation.1 | async-start | bytes 8192 | tf_op jit(solution)/shard_map/all_to_all | solution.py:64
  72.5 1.6 %convolution_bitcast_fusion = f32[32,4,8,128]{3,0,2,1:T(8,128)S(1)} fusion(f32[64,4,8,128]{3,2,1,0:T(8,128)S(1)} %fusion.7, f32[32,4,8]{0,2,1:T(8,128)S(1)} %select_reduce_fusion.1, f32[64,4,8]{0,2,1:T(8,128)S(1)} %copy.30, pred[32,64]{1,0:T(8,128)(4,1)S(1)} %copy.29), kind=kOutput, calls=%fused_computation.4 | convolution fusion | flops 100859904 | bytes 1587200 | tf_op jit(solution)/shard_map/rpkg,pkgd->rkgd/dot_general | solution.py:62
  74.1 1.1 %copy.35 = f32[32,4,8,128]{3,2,1,0:T(8,128)} copy(f32[32,4,8,128]{3,0,2,1:T(8,128)S(1)} %convolution_bitcast_fusion) | data formatting | bytes 1048576 | tf_op jit(solution)/shard_map/rpkg,pkgd->rkgd/transpose | solution.py:62
  75.2 2.8 %all-to-all-done.1 = f32[4,1,256]{2,1,0:T(1,128)S(1)} async-done(((f32[4,1,256]{2,1,0:T(1,128)}), f32[4,1,256]{2,1,0:T(1,128)S(1)}, u32[]{:S(2)}, u32[]{:S(2)}) %all-to-all-start.1) | async-done | bytes 4128 | tf_op jit(solution)/shard_map/all_to_all | solution.py:64
  78.1 4.1 %all-to-all-start.2 = ((f32[32,4,8,128]{3,2,1,0:T(8,128)}), f32[32,4,8,128]{3,2,1,0:T(8,128)S(1)}, u32[]{:S(2)}, u32[]{:S(2)}) async-start(f32[32,4,8,128]{3,2,1,0:T(8,128)} %copy.35), calls=%async_computation.2 | async-start | bytes 1048576 | tf_op jit(solution)/shard_map/all_to_all | solution.py:66
  82.1 0.5 broadcast.57
  82.6 0.7 reduce
  83.3 0.1 reshape.93
  83.4 0.1 copy.39
  83.5 0.7 reduce.1
  84.2 0.1 reshape.91
  84.3 0.1 copy.33
  84.5 0.1 copy.32
  84.6 0.1 multiply_reduce_fusion.1
  84.6 0.1 copy.40
  84.7 7.7 %all-to-all-done.2 = f32[32,4,8,128]{3,2,1,0:T(8,128)S(1)} async-done(((f32[32,4,8,128]{3,2,1,0:T(8,128)}), f32[32,4,8,128]{3,2,1,0:T(8,128)S(1)}, u32[]{:S(2)}, u32[]{:S(2)}) %all-to-all-start.2) | async-done | bytes 524320 | tf_op jit(solution)/shard_map/all_to_all | solution.py:66
  92.4 0.3 fusion.9
  92.8 0.7 fusion.19
  (3 shorter events, 0.0 us)
Async XLA Ops:
  1.6 47.3 %all-to-all-start = ((bf16[4,8,32,128]{3,2,1,0:T(8,128)(2,1)}), bf16[4,8,32,128]{3,2,1,0:T(8,128)(2,1)S(1)}, u32[]{:S(2)}, u32[]{:S(2)}) async-start(bf16[4,8,32,128]{3,2,1,0:T(8,128)(2,1)} %stack.2), calls=%async_computation | async-start | bytes 524288 | tf_op jit(solution)/shard_map/all_to_all | solution.py:22
  58.6 8.8 %all-to-all-start.3 = ((f32[4,1,256]{2,1,0:T(1,128)}), f32[4,1,256]{2,1,0:T(1,128)S(1)}, u32[]{:S(2)}, u32[]{:S(2)}) async-start(f32[4,1,256]{2,1,0:T(1,128)} %reshape.92), calls=%async_computation.3 | async-start | bytes 8192 | tf_op jit(solution)/shard_map/all_to_all | solution.py:65
  67.4 10.6 %all-to-all-start.1 = ((f32[4,1,256]{2,1,0:T(1,128)}), f32[4,1,256]{2,1,0:T(1,128)S(1)}, u32[]{:S(2)}, u32[]{:S(2)}) async-start(f32[4,1,256]{2,1,0:T(1,128)} %reshape.90), calls=%async_computation.1 | async-start | bytes 8192 | tf_op jit(solution)/shard_map/all_to_all | solution.py:64
  78.1 14.3 %all-to-all-start.2 = ((f32[32,4,8,128]{3,2,1,0:T(8,128)}), f32[32,4,8,128]{3,2,1,0:T(8,128)S(1)}, u32[]{:S(2)}, u32[]{:S(2)}) async-start(f32[32,4,8,128]{3,2,1,0:T(8,128)} %copy.35), calls=%async_computation.2 | async-start | bytes 1048576 | tf_op jit(solution)/shard_map/all_to_all | solution.py:66
